TPU v7x, 32 devices: a whole 2x2x4 slice. The times are simulated.
32 devices in a mesh: expert: 4 (over y, x), shard: 8 (over z, core).
Axes of the slice: x: 2, y: 2, z: 4, core: 2. Of those that a mesh axis runs over, the one named last changes fastest.
Arguments:
- tokens: bfloat16 [256, 6144], P(('expert', 'shard')), may hold values from -6 to 6
- norm_gain: float32 [6144], replicated, may hold values from 0.5 to 1.5
- routes: int32 [256, 2], P(('expert', 'shard')), may hold values from 0 to 3, all different within a row; in each aligned block of 8 rows (0 to 7, 8 to 15, ...) at most 4 rows name the same one
- gate_weights: float32 [256, 2], P(('expert', 'shard')), may hold values from 0.2 to 1
- capacity: int32 [4], replicated, may hold values from 2 to 4
- w_gate: bfloat16 [4, 6144, 8192], P('expert', None, 'shard'), may hold values from -0.078125 to 0.078125
- w_up: bfloat16 [4, 6144, 8192], P('expert', None, 'shard'), may hold values from -0.078125 to 0.078125
- w_down: bfloat16 [4, 8192, 6144], P('expert', 'shard'), may hold values from -0.0625 to 0.0625
Outputs:
- mixed_out: bfloat16 [256, 6144], P(('expert', 'shard'))
Inputs may be any that keep to these rules, and one draw needn't show every extreme that they name: `routes`: each row names 2 different experts; among the rows of one device no expert is named by more than 4 rows.
All inputs are finite; a program needn't handle non-finite values.
Results may differ from a plain program's by a relative error of at most 0.019.
Values may be sent and summed in bfloat16 or wider, within the bound.
A program may use at most 128 MiB of HBM per device.

v0:
```python
import jax
import jax.numpy as jnp
from jax import lax
from jax.sharding import PartitionSpec as P


def rms_norm(tokens, norm_gain):
    widened = tokens.astype(jnp.float32)
    mean_square = jnp.mean(widened * widened, axis=-1, keepdims=True)
    return (widened * lax.rsqrt(mean_square + 1e-05) * norm_gain).astype(jnp.bfloat16)


def slot_ranks(blocked):
    equal_ids = blocked[:, :, None, :, None] == blocked[:, None, :, None, :]
    shared = jnp.any(equal_ids, axis=4).astype(jnp.int32)
    per_block = blocked.shape[1]
    positions = jnp.arange(per_block, dtype=jnp.int32)
    earlier = (positions[None, :] < positions[:, None]).astype(jnp.int32)
    return jnp.sum(shared * earlier[None, :, :, None], axis=2)


def on_device(tokens, norm_gain, routes, gate_weights, capacity, w_gate, w_up, w_down):
    normed = rms_norm(tokens, norm_gain)
    tok_count = tokens.shape[0]
    expert_count = capacity.shape[0]
    slot_depth = max(tok_count // 2, tok_count * routes.shape[1] // expert_count)
    slot_rank = slot_ranks(routes[None])[0]
    expert_ids = jnp.arange(expert_count, dtype=jnp.int32)
    is_expert = routes[:, :, None] == expert_ids
    limit_rows = jnp.sum(jnp.where(is_expert, capacity, 0), axis=-1)
    kept_mask = slot_rank < limit_rows
    slot_ids = jnp.arange(slot_depth, dtype=jnp.int32)
    matched = (
        is_expert[:, :, :, None]
        & (slot_rank[:, :, None, None] == slot_ids)
        & kept_mask[:, :, None, None]
    )
    picker = jnp.sum(matched.astype(jnp.float32), axis=1).astype(jnp.bfloat16)
    buffers = jnp.einsum("tej,td->ejd", picker, normed, preferred_element_type=jnp.float32).astype(
        jnp.bfloat16
    )
    combine = jnp.sum(jnp.where(matched, gate_weights[:, :, None, None], jnp.float32(0.0)), axis=1)
    gate_proj = w_gate[0]
    up_proj = w_up[0]
    down_proj = w_down[0]
    arrived = lax.all_to_all(buffers, "expert", split_axis=0, concat_axis=0, tiled=True)
    slot_rows = lax.all_gather(arrived[None], "shard", axis=0, tiled=True)
    row_shape = slot_rows.shape
    flat_rows = slot_rows.reshape(-1, row_shape[-1])
    gate_val = jnp.dot(flat_rows, gate_proj, preferred_element_type=jnp.float32)
    up_val = jnp.dot(flat_rows, up_proj, preferred_element_type=jnp.float32)
    hidden = (jax.nn.silu(gate_val) * up_val).astype(jnp.bfloat16)
    partial_out = jnp.dot(hidden, down_proj, preferred_element_type=jnp.float32)
    partial_value = partial_out.reshape(row_shape[:-1] + (down_proj.shape[1],))
    rounded_parts = partial_value.astype(jnp.bfloat16)
    pieces = lax.all_to_all(
        lax.all_to_all(rounded_parts, "expert", split_axis=1, concat_axis=1, tiled=True),
        "shard",
        split_axis=0,
        concat_axis=0,
        tiled=True,
    )
    returned = jnp.sum(pieces.astype(jnp.float32), axis=0).astype(jnp.bfloat16)
    mixed_out = jnp.einsum(
        "tej,ejd->td", combine, returned.astype(jnp.float32), precision=lax.Precision.HIGHEST
    )
    return mixed_out.astype(jnp.bfloat16)


def solution(mesh):
    in_specs = (
        P(("expert", "shard"), None),
        P(),
        P(("expert", "shard"), None),
        P(("expert", "shard"), None),
        P(),
        P("expert", None, "shard"),
        P("expert", None, "shard"),
        P("expert", "shard", None),
    )
    out_specs = P(("expert", "shard"), None)
    return jax.shard_map(
        on_device, mesh=mesh, in_specs=in_specs, out_specs=out_specs, check_vma=False
    )
```

profile of v0, /device:TPU:0, one launch (start us, length us, event | category | flops | bytes accessed | tf_op | source)
XLA Modules:
  0.0 144.9 jit_solution(16787414954088235093)
XLA Ops:
  6.5 0.0 all-gather.3.cloned.1.call-start
  6.5 1.1 fusion.17
  7.6 0.8 compare_reduce_fusion
  8.4 0.8 select_reduce_fusion.2
  9.2 0.1 select_reduce_fusion.1
  9.4 0.7 iota_compare_fusion
  10.1 0.7 convert_reduce_fusion
  10.8 1.1 convolution_convert_fusion
  11.9 10.6 %all_to_all.15 = bf16[4,4,6144]{2,1,0:T(4,128)(2,1)} all-to-all(bf16[4,4,6144]{2,1,0:T(4,128)(2,1)S(1)} %convolution_convert_fusion), channel_id=1, replica_groups=mesh['expert'=4,'shard'=8] {'expert'}, dimensions={0} | all-to-all | bytes 393216 | tf_op jit(solution)/shard_map/all_to_all | solution.py:46
  22.6 0.0 all-gather.3.cloned.1.call-update
  22.6 25.0 %all-gather.3.cloned.1.call-done = bf16[32,4,6144]{2,1,0:T(4,128)(2,1)} async-done(((bf16[4,4,6144]{2,1,0:T(4,128)(2,1)}), bf16[32,4,6144]{2,1,0:T(4,128)(2,1)}) %all-gather.3.cloned.1.call-update) | async-done | bytes 1572880 | tf_op jit(solution)/shard_map/all_gather | solution.py:47
  47.6 2.7 %reshape.66 = bf16[128,6144]{1,0:T(8,128)(2,1)S(1)} reshape(bf16[32,4,6144]{2,1,0:T(4,128)(2,1)} %all-gather.3.cloned.1.call-done) | data formatting | bytes 3145728 | tf_op jit(solution)/shard_map/reshape | solution.py:49
  50.3 6.5 %fusion.4 = f32[128,1024]{1,0:T(8,128)S(1)} fusion(bf16[128,6144]{1,0:T(8,128)(2,1)S(1)} %reshape.66, bf16[1,6144,1024]{2,1,0:T(8,128)(2,1)} %param.13), kind=kOutput, calls=%fused_computation.4 | convolution fusion | flops 1610612736 | bytes 14680064 | tf_op jit(solution)/shard_map/dot_general | solution.py:50
  56.8 6.6 %fusion.13 = bf16[128,1024]{1,0:T(8,128)(2,1)S(1)} fusion(bf16[128,6144]{1,0:T(8,128)(2,1)S(1)} %reshape.66, bf16[1,6144,1024]{2,1,0:T(8,128)(2,1)} %param.14, f32[128,1024]{1,0:T(8,128)S(1)} %fusion.4), kind=kOutput, calls=%fused_computation.11 | convolution fusion | flops 1611399168 | bytes 14942208 | tf_op jit(solution)/shard_map/dot_general | solution.py:51
  63.3 0.1 dot_general.20
  63.4 7.9 %fusion.6 = bf16[8,4,4,6144]{3,2,0,1:T(4,128)(2,1)S(1)} fusion(bf16[1,1024,6144]{2,1,0:T(8,128)(2,1)} %param.15, bf16[8,4,4,1024]{3,2,1,0:T(4,128)(2,1)S(1)} %dot_general.20), kind=kOutput, calls=%fused_computation.6 | convolution fusion | flops 1611399168 | bytes 14417920 | tf_op jit(solution)/shard_map/dot_general | solution.py:53
  71.4 23.6 %all_to_all.16 = bf16[8,4,4,6144]{3,2,0,1:T(4,128)(2,1)S(1)} all-to-all(bf16[8,4,4,6144]{3,2,0,1:T(4,128)(2,1)S(1)} %fusion.6), channel_id=1, replica_groups=mesh['expert'=4,'shard'=8] {'expert'}, dimensions={1} | all-to-all | bytes 3145728 | tf_op jit(solution)/shard_map/all_to_all | solution.py:57
  95.0 0.7 copy.24
  95.7 40.4 %all_to_all.17 = bf16[8,4,4,6144]{3,2,1,0:T(4,128)(2,1)S(1)} all-to-all(bf16[8,4,4,6144]{3,2,1,0:T(4,128)(2,1)S(1)} %copy.24), channel_id=1, replica_groups=mesh['expert'=4,'shard'=8] {'shard'}, dimensions={0} | all-to-all | bytes 3145728 | tf_op jit(solution)/shard_map/all_to_all | solution.py:56
  136.1 0.9 reduce_sum.62
  137.0 1.0 fusion.9
  (3 shorter events, 0.0 us)
Async XLA Ops:
  6.5 41.0 %all-gather.3.cloned.1.call-start = ((), (), s32[]{:S(2)}) async-start(), calls=%async_computation.3 | async-start | bytes 1769472 | tf_op jit(solution)/shard_map/all_gather | solution.py:47
Sparse Core Ops, SparseCore 0:
  22.7 24.7 all-gather.2
where the time goes:
time: 145 us
  blocking collectives  74.7 us (52%)
  waiting for transfers between devices  25 us (17%)
  matrix products  23.1 us (16%)
  between operations  13.5 us (9%)
  other arithmetic  5.17 us (4%)
  local copies, waits for them, and re-layouts  3.49 us (2%)
    all_to_all x1, blocking collectives, on_device(): lax.all_to_all(lax.all_to_all(rounded_parts, 'expert', split_axis=1, conc...  40.4 us
    all_gather x1, waiting for transfers between devices, on_device(): slot_rows = lax.all_gather(arrived[None], 'shard', axis=0, tiled=True)  25 us
    all_to_all x1, blocking collectives, on_device(): lax.all_to_all(rounded_parts, 'expert', split_axis=1, concat_axis=1, tile...  23.6 us
    all_to_all x1, blocking collectives, on_device(): lax.all_to_all(buffers, 'expert', split_axis=0, concat_axis=0, tiled=True)  10.6 us
    dot_general x1, matrix products, on_device(): partial_out = jnp.dot(hidden, down_proj, preferred_element_type=jnp.float32)  7.91 us
    dot_general x1, matrix products, on_device(): up_val = jnp.dot(flat_rows, up_proj, preferred_element_type=jnp.float32)  6.57 us
    dot_general x1, matrix products, on_device(): gate_val = jnp.dot(flat_rows, gate_proj, preferred_element_type=jnp.float32)  6.49 us
  transfers between devices with their start and end apart: 1, of which 1 were waited for; matrix products, arithmetic and copies ran while one was open for 0% of the time, Pallas kernels for 0%

commit v1 on v0

--- a/solution.py
+++ b/solution.py
@@ -54,7 +54,12 @@
     partial_value = partial_out.reshape(row_shape[:-1] + (down_proj.shape[1],))
     rounded_parts = partial_value.astype(jnp.bfloat16)
     pieces = lax.all_to_all(
-        lax.all_to_all(rounded_parts, "expert", split_axis=1, concat_axis=1, tiled=True),
+        jnp.concatenate(
+            lax.all_to_all(
+                jnp.stack(jnp.split(rounded_parts, lax.axis_size("expert"), axis=1)), "expert", 0, 0
+            ),
+            axis=1,
+        ),
         "shard",
         split_axis=0,
         concat_axis=0,

time: 145 us -> 145 us (level)
  no operation moved by 1% of the time
where the time goes in v1:
time: 145 us; the launch traced here: 144 us
  blocking collectives  74.7 us (52%)
  waiting for transfers between devices  25 us (17%)
  matrix products  21.7 us (15%)
  between operations  13.5 us (9%)
  other arithmetic  5.37 us (4%)
  local copies, waits for them, and re-layouts  4.11 us (3%)
    all_to_all x1, blocking collectives, on_device(): lax.all_to_all(jnp.concatenate(lax.all_to_all(jnp.stack(jnp.split(rounded...  40.4 us
    all_gather x1, waiting for transfers between devices, on_device(): slot_rows = lax.all_gather(arrived[None], 'shard', axis=0, tiled=True)  25 us
    all_to_all x1, blocking collectives, on_device(): lax.all_to_all(jnp.stack(jnp.split(rounded_parts, lax.axis_size('expert')...  23.6 us
    all_to_all x1, blocking collectives, on_device(): lax.all_to_all(buffers, 'expert', split_axis=0, concat_axis=0, tiled=True)  10.6 us
    dot_general x1, matrix products, on_device(): up_val = jnp.dot(flat_rows, up_proj, preferred_element_type=jnp.float32)  6.57 us
    dot_general x1, matrix products, on_device(): gate_val = jnp.dot(flat_rows, gate_proj, preferred_element_type=jnp.float32)  6.49 us
    dot_general x1, matrix products, on_device(): partial_out = jnp.dot(hidden, down_proj, preferred_element_type=jnp.float32)  6.48 us
  transfers between devices with their start and end apart: 1, of which 1 were waited for; matrix products, arithmetic and copies ran while one was open for 0% of the time, Pallas kernels for 0%

profile of v1, /device:TPU:0, one launch (start us, length us, event | category | flops | bytes accessed | tf_op | source)
XLA Modules:
  0.0 144.3 jit_solution(18145614336359356005)
XLA Ops:
  6.5 0.0 all-gather.3.cloned.1.call-start
  6.5 1.1 fusion.17
  7.6 0.8 compare_reduce_fusion
  8.4 0.8 select_reduce_fusion.2
  9.2 0.1 select_reduce_fusion.1
  9.4 0.7 iota_compare_fusion
  10.1 0.7 convert_reduce_fusion
  10.8 1.1 convolution_convert_fusion
  11.9 10.6 %all_to_all.15 = bf16[4,4,6144]{2,1,0:T(4,128)(2,1)} all-to-all(bf16[4,4,6144]{2,1,0:T(4,128)(2,1)S(1)} %convolution_convert_fusion), channel_id=1, replica_groups=mesh['expert'=4,'shard'=8] {'expert'}, dimensions={0} | all-to-all | bytes 393216 | tf_op jit(solution)/shard_map/all_to_all | solution.py:46
  22.6 0.0 all-gather.3.cloned.1.call-update
  22.6 25.0 %all-gather.3.cloned.1.call-done = bf16[32,4,6144]{2,1,0:T(4,128)(2,1)} async-done(((bf16[4,4,6144]{2,1,0:T(4,128)(2,1)}), bf16[32,4,6144]{2,1,0:T(4,128)(2,1)}) %all-gather.3.cloned.1.call-update) | async-done | bytes 1572880 | tf_op jit(solution)/shard_map/all_gather | solution.py:47
  47.6 2.7 %reshape.72 = bf16[128,6144]{1,0:T(8,128)(2,1)S(1)} reshape(bf16[32,4,6144]{2,1,0:T(4,128)(2,1)} %all-gather.3.cloned.1.call-done) | data formatting | bytes 3145728 | tf_op jit(solution)/shard_map/reshape | solution.py:49
  50.3 6.5 %fusion.4 = f32[128,1024]{1,0:T(8,128)S(1)} fusion(bf16[128,6144]{1,0:T(8,128)(2,1)S(1)} %reshape.72, bf16[1,6144,1024]{2,1,0:T(8,128)(2,1)} %param.13), kind=kOutput, calls=%fused_computation.4 | convolution fusion | flops 1610612736 | bytes 14680064 | tf_op jit(solution)/shard_map/dot_general | solution.py:50
  56.8 6.6 %fusion.13 = bf16[128,1024]{1,0:T(8,128)(2,1)S(1)} fusion(bf16[128,6144]{1,0:T(8,128)(2,1)S(1)} %reshape.72, bf16[1,6144,1024]{2,1,0:T(8,128)(2,1)} %param.14, f32[128,1024]{1,0:T(8,128)S(1)} %fusion.4), kind=kOutput, calls=%fused_computation.12 | convolution fusion | flops 1611399168 | bytes 14942208 | tf_op jit(solution)/shard_map/dot_general | solution.py:51
  63.3 0.1 dot_general.20
  63.4 6.5 %fusion.6 = bf16[8,4,4,6144]{3,0,2,1:T(8,128)(2,1)S(1)} fusion(bf16[1,1024,6144]{2,1,0:T(8,128)(2,1)} %param.15, bf16[8,4,4,1024]{3,2,1,0:T(4,128)(2,1)S(1)} %dot_general.20), kind=kOutput, calls=%fused_computation.6 | convolution fusion | flops 1611399168 | bytes 14417920 | tf_op jit(solution)/shard_map/dot_general | solution.py:53
  69.9 0.1 slice_bitcast_fusion.3
  70.0 0.2 pad_maximum_fusion
  70.3 23.6 %all_to_all.16 = bf16[4,8,1,4,6144]{4,1,3,2,0:T(8,128)(2,1)S(1)} all-to-all(bf16[4,8,1,4,6144]{4,1,3,2,0:T(8,128)(2,1)S(1)} %pad_maximum_fusion), channel_id=1, replica_groups=mesh['expert'=4,'shard'=8] {'expert'}, dimensions={0} | all-to-all | bytes 3145728 | tf_op jit(solution)/shard_map/all_to_all | solution.py:58
  93.8 1.2 copy.21
  95.1 40.4 %all_to_all.17 = bf16[8,4,4,6144]{3,2,1,0:T(4,128)(2,1)S(1)} all-to-all(bf16[8,4,4,6144]{3,2,1,0:T(4,128)(2,1)S(1)} %copy.21), channel_id=1, replica_groups=mesh['expert'=4,'shard'=8] {'shard'}, dimensions={0} | all-to-all | bytes 3145728 | tf_op jit(solution)/shard_map/all_to_all | solution.py:56
  135.5 0.9 reduce_sum.62
  136.4 1.0 fusion.9
  (3 shorter events, 0.0 us)
Async XLA Ops:
  6.5 41.0 %all-gather.3.cloned.1.call-start = ((), (), s32[]{:S(2)}) async-start(), calls=%async_computation.3 | async-start | bytes 1769472 | tf_op jit(solution)/shard_map/all_gather | solution.py:47
Sparse Core Ops, SparseCore 0:
  22.7 24.7 all-gather.2
